TPU v7x, 32 devices: a whole 2x2x4 slice. The times are simulated.
32 devices in a mesh: groups: 2 (over y), ga: 16 (over z, x, core).
Axes of the slice: x: 2, y: 2, z: 4, core: 2. Of those that a mesh axis runs over, the one named last changes fastest.
Arguments:
- occupied: float32 [2, 1024, 12288], P(None, None, 'ga'), may hold values from -0.0546875 to 0.0546875
- residual: float32 [4, 2, 128, 12288], P('groups', None, None, 'ga'), parts along dimension 0, may hold values from -6 to 6
- old_direction: float32 [4, 2, 128, 12288], P('groups', None, None, 'ga'), parts along dimension 0, may hold values from -6 to 6
- kin_ratio: float32 [12288], P('ga'), may hold values from 0.06 to 5, as said below
- old_dot: float32 [4, 128], P('groups'), parts along dimension 0, may hold values from 6144 to 24576
Outputs:
- direction: float32 [4, 2, 128, 12288], P('groups', None, None, 'ga'), parts along dimension 0
- dot_new: float32 [4, 128], P('groups'), parts along dimension 0
There are 2 independent parts, one for each index of `groups`. A program takes and returns all parts, laid end to end along the dimension named above; an argument that names none is the same for every part. Nothing has to cross between parts.
Inputs may be any that keep to these rules, and one draw needn't show every extreme that they name: `kin_ratio`: positive; grows with the plane-wave index on average and varies from one plane wave to the next.
All inputs are finite; a program needn't handle non-finite values.
Results may differ from a plain program's by a relative error of at most 0.000056.
Values sent between devices are 32-bit elements; how exact they have to be, the bound alone decides.
No kernel may reach another device: no remote copies, remote signals or barrier semaphores. Data moves between devices by JAX's collectives and lax.ppermute only.
A program may use at most 64 MiB of HBM per device.

v0:
```python
import jax
import jax.numpy as jnp
from jax import lax
from jax.sharding import PartitionSpec as P

highest = lax.Precision.HIGHEST


def teter_factor(ratio):
    numerator = 27.0 + 18.0 * ratio + 12.0 * ratio**2 + 8.0 * ratio**3
    return numerator / (numerator + 16.0 * ratio**4)


def margins(occupied, vectors):
    products = jnp.einsum("hng,pcbg->phcnb", occupied, vectors, precision=highest)
    real_part = products[:, 0, 0] + products[:, 1, 1]
    imag_part = products[:, 0, 1] - products[:, 1, 0]
    return jnp.stack([real_part, imag_part], axis=1)


def correction(summed, occ_rows):
    real_part = summed[:, 0]
    imag_part = summed[:, 1]
    coefficient = jnp.stack(
        [jnp.stack([real_part, -imag_part], axis=1), jnp.stack([imag_part, real_part], axis=1)],
        axis=1,
    )
    return jnp.einsum("pchnb,hng->pcbg", coefficient, occ_rows, precision=highest)


def on_device(occupied, residual, old_direction, kin_ratio, old_dot):
    factor = teter_factor(kin_ratio)
    first = margins(occupied, residual)
    first_total = lax.psum(first, "ga")
    gradient = residual - correction(first_total, occupied)
    precond = factor * gradient
    local_dot = jnp.sum(factor * (gradient[:, 0] ** 2 + gradient[:, 1] ** 2), axis=-1)
    second = margins(occupied, precond)
    second_total, dot_new = lax.psum((second, local_dot), "ga")
    projected = precond - correction(second_total, occupied)
    direction = projected + (dot_new / old_dot)[:, None, :, None] * old_direction
    return (direction, dot_new)


def solution(mesh):
    placed = (
        P(None, None, "ga"),
        P("groups", None, None, "ga"),
        P("groups", None, None, "ga"),
        P("ga"),
        P("groups", None),
    )
    return jax.shard_map(
        on_device,
        mesh=mesh,
        in_specs=placed,
        out_specs=(P("groups", None, None, "ga"), P("groups", None)),
        check_vma=False,
    )
```

profile of v0, /device:TPU:0, one launch (start us, length us, event | category | flops | bytes accessed | tf_op | source)
XLA Modules:
  0.0 279.0 jit_solution(1500607859630223277)
XLA Ops:
  7.2 0.0 all-reduce.3.cloned.1.call-start
  7.2 13.1 %fusion.10 = f32[2,2,2,1024,128]{3,4,1,2,0:T(8,128)S(1)} fusion(f32[2,1024,768]{2,1,0:T(8,128)} %param.5, f32[2,2,128,768]{3,2,1,0:T(8,128)} %param.6), kind=kOutput, calls=%fused_computation.12 | convolution fusion | flops 9663676416 | bytes 12058624 | tf_op jit(solution)/shard_map/hng,pcbg->phcnb/dot_general | solution.py:15
  20.4 0.2 fusion.31
  20.5 0.2 fusion.33
  20.7 1.4 pad_maximum_fusion.2
  22.2 0.2 all-reduce.5.cloned.1.call-start
  22.4 0.4 copy-done.3
  22.8 100.4 %all-reduce.3.cloned.1.call-done = f32[2,2,1024,128]{2,3,0,1:T(8,128)} async-done(((f32[2,2,1024,128]{2,3,0,1:T(8,128)}), f32[2,2,1024,128]{2,3,0,1:T(8,128)}) %all-reduce.3.cloned.1.call-update) | async-done | bytes 2097168 | tf_op jit(solution)/shard_map/psum | solution.py:34
  123.2 1.9 slice_negate_fusion.1
  125.2 0.5 maximum_bitcast_fusion
  125.7 0.9 copy-done
  126.6 16.2 %bitcast_subtract_fusion.1 = f32[2,2,128,768]{3,2,1,0:T(8,128)S(1)} fusion(f32[2,2,128,768]{3,2,1,0:T(8,128)S(1)} %copy-done, f32[2,1024,768]{2,1,0:T(8,128)} %param.5, f32[2,1,2,1024,128]{3,4,0,2,1:T(8,128)S(1)} %get-tuple-element.11, f32[2,1,2,1024,128]{3,4,0,2,1:T(8,128)S(1)} %get-tuple-element.10), kind=kOutput, calls=%fused_computation.24 | convolution fusion | flops 9665118208 | bytes 13631488 | tf_op jit(solution)/shard_map/pchnb,hng->pcbg/dot_general | solution.py:28
  142.8 10.2 %fusion.13 = f32[2,2,2,1024,128]{3,4,1,2,0:T(8,128)S(1)} fusion(f32[2,1024,768]{2,1,0:T(8,128)S(1)} %bitcast.84, f32[2,2,128,768]{3,2,1,0:T(8,128)S(1)} %bitcast_subtract_fusion.1, f32[768]{0:T(1024)S(1)} %add_divide_fusion), kind=kOutput, calls=%fused_computation.13 | convolution fusion | flops 9664069632 | bytes 12061696 | tf_op jit(solution)/shard_map/hng,pcbg->phcnb/dot_general | solution.py:15
  153.0 0.2 fusion.28
  153.1 0.2 fusion.30
  153.3 1.4 pad_maximum_fusion.3
  154.7 0.0 all-reduce.5.cloned.1.call-update
  154.8 0.2 fusion.37
  155.0 31.1 %psum.23 = f32[2,128]{1,0:T(2,128)S(1)} all-reduce(f32[2,128]{1,0:T(2,128)S(1)} %fusion.37), channel_id=1, replica_groups=mesh['groups'=2,'ga'=16] {'ga'}, use_global_device_ids=true, to_apply=%region_3.0 | all-reduce | flops 256 | bytes 2048 | tf_op jit(solution)/shard_map/psum | solution.py:39
  186.1 66.3 %all-reduce.5.cloned.1.call-done = f32[2,2,1024,128]{2,3,0,1:T(8,128)} async-done(((f32[2,2,1024,128]{2,3,0,1:T(8,128)}), f32[2,2,1024,128]{2,3,0,1:T(8,128)}) %all-reduce.5.cloned.1.call-update) | async-done | bytes 2097168 | tf_op jit(solution)/shard_map/psum | solution.py:39
  252.5 1.9 slice_negate_fusion
  254.4 0.5 maximum_bitcast_fusion.2
  254.9 0.9 copy-done.1
  255.8 16.4 %fusion.18 = f32[2,2,128,768]{3,2,1,0:T(8,128)} fusion(f32[2,2,128,768]{3,2,1,0:T(8,128)S(1)} %copy-done.1, f32[2,1024,768]{2,1,0:T(8,128)} %param.5, f32[2,2,128,768]{3,2,1,0:T(8,128)S(1)} %bitcast_subtract_fusion.1, f32[2,128]{1,0:T(2,128)S(1)} %div.7, f32[768]{0:T(1024)S(1)} %add_divide_fusion, f32[2,1,2,1024,128]{3,4,0,2,1:T(8,128)S(1)} %get-tuple-element.9, ...), kind=kOutput, calls=%fused_computation.23 | convolution fusion | flops 9666297856 | bytes 15208448 | tf_op jit(solution)/shard_map/pchnb,hng->pcbg/dot_general | solution.py:28
  (15 shorter events, 0.1 us)
Async XLA Ops:
  7.2 116.1 %all-reduce.3.cloned.1.call-start = ((), (), s32[]{:S(2)}) async-start(), calls=%async_computation | async-start | bytes 4194304 | tf_op jit(solution)/shard_map/psum | solution.py:34
  22.1 0.7 copy-start.3
  22.2 230.3 %all-reduce.5.cloned.1.call-start = ((), (), s32[]{:S(2)}) async-start(), calls=%async_computation.1 | async-start | bytes 4194304 | tf_op jit(solution)/shard_map/psum | solution.py:39
  125.1 1.4 copy-start
  125.1 17.6 %slice-start = ((s8[6291456]{0:T(1024)(128)(4,1)}), s8[4194304]{0:T(1024)(128)(4,1)S(1)}, s32[]{:S(2)}) async-start(s8[6291456]{0:T(1024)(128)(4,1)} %bitcast.83), calls=%async_computation.2 | async-start | bytes 8388608
  126.5 16.2 %slice-start.1 = ((s8[6291456]{0:T(1024)(128)(4,1)}), s8[2097152]{0:T(1024)(128)(4,1)S(1)}, s32[]{:S(2)}) async-start(s8[6291456]{0:T(1024)(128)(4,1)} %bitcast.83), calls=%async_computation.3 | async-start | bytes 4194304
  154.7 31.4 %copy-start.4 = (f32[2,128]{1,0:T(2,128)S(1)}, f32[2,128]{1,0:T(2,128)}, u32[]{:S(2)}) copy-start(f32[2,128]{1,0:T(2,128)} %param.9) | copy-start | bytes 3076
  186.1 68.3 %copy-start.2 = (f32[2,128]{1,0:T(2,128)}, f32[2,128]{1,0:T(2,128)S(1)}, u32[]{:S(2)}) copy-start(f32[2,128]{1,0:T(2,128)S(1)} %psum.23) | copy-start | bytes 3076
  254.4 1.4 copy-start.1
Sparse Core Ops, SparseCore 0:
  22.3 100.8 all-reduce.2
  154.9 97.5 all-reduce.4
where the time goes:
time: 279 us
  waiting for transfers between devices  167 us (60%)
  matrix products  55.9 us (20%)
  blocking collectives  31.1 us (11%)
  between operations  14.2 us (5%)
  other arithmetic  8.56 us (3%)
    psum x1, waiting for transfers between devices, on_device(): first_total = lax.psum(first, 'ga')  100 us
    psum x1, waiting for transfers between devices, on_device(): second_total, dot_new = lax.psum((second, local_dot), 'ga')  66.3 us
    dot_general x2, matrix products, correction(): jnp.einsum('pchnb,hng->pcbg', coefficient, occ_rows, precision=highest)  32.6 us
    psum x1, blocking collectives, on_device(): second_total, dot_new = lax.psum((second, local_dot), 'ga')  31.1 us
    dot_general x2, matrix products, margins(): jnp.einsum('hng,pcbg->phcnb', occupied, vectors, precision=highest)  23.3 us
  transfers between devices with their start and end apart: 2, of which 2 were waited for; matrix products, arithmetic and copies ran while one was open for 0% of the time, Pallas kernels for 0%

commit v1 on v0

--- a/solution.py
+++ b/solution.py
@@ -31,7 +31,11 @@
 def on_device(occupied, residual, old_direction, kin_ratio, old_dot):
     factor = teter_factor(kin_ratio)
     first = margins(occupied, residual)
-    first_total = lax.psum(first, "ga")
+    first_total = first
+    for hop in (1, 2, 4, 8):
+        first_total = first_total + lax.ppermute(
+            first_total, "ga", [(dev, dev ^ hop) for dev in range(16)]
+        )
     gradient = residual - correction(first_total, occupied)
     precond = factor * gradient
     local_dot = jnp.sum(factor * (gradient[:, 0] ** 2 + gradient[:, 1] ** 2), axis=-1)

time: 279 us -> 368 us (1.32)
  waiting for transfers between devices: 167 us -> 250 us
  starting transfers between devices: 0.26 us -> 8.02 us
  matrix products: 55.9 us -> 50.6 us
    ppermute x0 -> x4, waiting for transfers between devices: none -> 184 us  [on_device(): lax.ppermute(first_total, 'ga', [(dev, dev ^ hop) for dev in range(16)])]
    psum x1 -> x0, waiting for transfers between devices: 100 us -> none  [on_device(): first_total = lax.psum(first, 'ga')]
    ppermute x0 -> x4, starting transfers between devices: none -> 7.99 us  [on_device(): lax.ppermute(first_total, 'ga', [(dev, dev ^ hop) for dev in range(16)])]
    dot_general x2, matrix products: 32.6 us -> 27.1 us  [correction(): jnp.einsum('pchnb,hng->pcbg', coefficient, occ_rows, precision=highest)]
  transfers between devices with their start and end apart: 2 -> 5, of which waited for: 2 -> 5; matrix products, arithmetic and copies ran while one was open for 0% -> 0% of each run, Pallas kernels for 0% -> 0%
where the time goes in v1:
time: 368 us; the launch traced here: 367 us
  waiting for transfers between devices  250 us (68%)
  matrix products  50.6 us (14%)
  blocking collectives  33.6 us (9%)
  between operations  14.2 us (4%)
  starting transfers between devices  8.02 us (2%)
  other arithmetic  7.91 us (2%)
    ppermute x4, waiting for transfers between devices, on_device(): lax.ppermute(first_total, 'ga', [(dev, dev ^ hop) for dev in range(16)])  184 us
    psum x1, waiting for transfers between devices, on_device(): second_total, dot_new = lax.psum((second, local_dot), 'ga')  65.5 us
    psum x1, blocking collectives, on_device(): second_total, dot_new = lax.psum((second, local_dot), 'ga')  33.6 us
    dot_general x2, matrix products, correction(): jnp.einsum('pchnb,hng->pcbg', coefficient, occ_rows, precision=highest)  27.1 us
    dot_general x2, matrix products, margins(): jnp.einsum('hng,pcbg->phcnb', occupied, vectors, precision=highest)  23.5 us
    ppermute x4, starting transfers between devices, on_device(): lax.ppermute(first_total, 'ga', [(dev, dev ^ hop) for dev in range(16)])  7.99 us
  transfers between devices with their start and end apart: 5, of which 5 were waited for; matrix products, arithmetic and copies ran while one was open for 0% of the time, Pallas kernels for 0%

profile of v1, /device:TPU:0, one launch (start us, length us, event | category | flops | bytes accessed | tf_op | source)
XLA Modules:
  0.0 367.4 jit_solution(79875686517020440)
XLA Ops:
  7.2 13.3 %fusion.10 = f32[2,2,2,1024,128]{3,4,1,2,0:T(8,128)S(1)} fusion(f32[2,1024,768]{2,1,0:T(8,128)} %param.5, f32[2,2,128,768]{3,2,1,0:T(8,128)} %param.6), kind=kOutput, calls=%fused_computation.12 | convolution fusion | flops 9663676416 | bytes 12058624 | tf_op jit(solution)/shard_map/hng,pcbg->phcnb/dot_general | solution.py:15
  21.2 0.6 collective-permute-start
  21.7 3.8 %collective-permute-done = f32[2,2,1024,128]{2,3,0,1:T(8,128)S(1)} collective-permute-done((f32[2,2,1024,128]{2,3,0,1:T(8,128)S(1)}, f32[2,2,1024,128]{2,3,0,1:T(8,128)S(1)}, u32[]{:S(2)}, u32[]{:S(2)}) %collective-permute-start) | collective-permute-done | bytes 2097184 | tf_op jit(solution)/shard_map/ppermute | solution.py:36
  25.5 0.4 fusion.43
  25.9 2.9 collective-permute-start.1
  28.8 45.9 %collective-permute-done.1 = f32[2,2,1024,128]{2,3,0,1:T(8,128)S(1)} collective-permute-done((f32[2,2,1024,128]{2,3,0,1:T(8,128)S(1)}, f32[2,2,1024,128]{2,3,0,1:T(8,128)S(1)}, u32[]{:S(2)}, u32[]{:S(2)}) %collective-permute-start.1) | collective-permute-done | bytes 2097184 | tf_op jit(solution)/shard_map/ppermute | solution.py:36
  74.7 0.9 fusion.44
  75.6 1.9 collective-permute-start.2
  77.5 45.3 %collective-permute-done.2 = f32[2,2,1024,128]{2,3,0,1:T(8,128)S(1)} collective-permute-done((f32[2,2,1024,128]{2,3,0,1:T(8,128)S(1)}, f32[2,2,1024,128]{2,3,0,1:T(8,128)S(1)}, u32[]{:S(2)}, u32[]{:S(2)}) %collective-permute-start.2) | collective-permute-done | bytes 2097184 | tf_op jit(solution)/shard_map/ppermute | solution.py:36
  123.2 2.6 collective-permute-start.3
  125.8 89.5 %collective-permute-done.3 = f32[2,2,1024,128]{2,3,0,1:T(8,128)S(1)} collective-permute-done((f32[2,2,1024,128]{2,3,0,1:T(8,128)S(1)}, f32[2,2,1024,128]{2,3,0,1:T(8,128)S(1)}, u32[]{:S(2)}, u32[]{:S(2)}) %collective-permute-start.3) | collective-permute-done | bytes 2097184 | tf_op jit(solution)/shard_map/ppermute | solution.py:36
  216.1 0.5 maximum_bitcast_fusion
  216.6 0.9 slice-done
  217.5 0.8 slice-done.1
  218.3 0.5 copy-done
  218.8 10.7 %bitcast_subtract_fusion.1 = f32[2,2,128,768]{3,2,1,0:T(8,128)S(1)} fusion(f32[2,2,128,768]{3,2,1,0:T(8,128)S(1)} %copy-done, f32[2,1024,768]{2,1,0:T(8,128)S(1)} %bitcast.84, f32[2,1,2,1024,128]{3,4,0,2,1:T(8,128)S(1)} %get-tuple-element.11, f32[2,1,2,1024,128]{3,4,0,2,1:T(8,128)S(1)} %get-tuple-element.10), kind=kOutput, calls=%fused_computation.24 | convolution fusion | flops 9665118208 | bytes 13631488 | tf_op jit(solution)/shard_map/pchnb,hng->pcbg/dot_general | solution.py:28
  229.5 10.2 %fusion.13 = f32[2,2,2,1024,128]{3,4,1,2,0:T(8,128)S(1)} fusion(f32[2,1024,768]{2,1,0:T(8,128)S(1)} %bitcast.84, f32[2,2,128,768]{3,2,1,0:T(8,128)S(1)} %bitcast_subtract_fusion.1, f32[768]{0:T(1024)S(1)} %add_divide_fusion), kind=kOutput, calls=%fused_computation.13 | convolution fusion | flops 9664069632 | bytes 12061696 | tf_op jit(solution)/shard_map/hng,pcbg->phcnb/dot_general | solution.py:15
  240.0 1.5 pad_maximum_fusion.3
  241.7 33.6 %psum.15 = f32[2,128]{1,0:T(2,128)S(1)} all-reduce(f32[2,128]{1,0:T(2,128)S(1)} %fusion.37), channel_id=1, replica_groups=mesh['groups'=2,'ga'=16] {'ga'}, use_global_device_ids=true, to_apply=%region_2.0 | all-reduce | flops 256 | bytes 2048 | tf_op jit(solution)/shard_map/psum | solution.py:43
  275.3 65.5 %all-reduce.2.cloned.1.call-done = f32[2,2,1024,128]{2,3,0,1:T(8,128)} async-done(((f32[2,2,1024,128]{2,3,0,1:T(8,128)}), f32[2,2,1024,128]{2,3,0,1:T(8,128)}) %all-reduce.2.cloned.1.call-update) | async-done | bytes 2097168 | tf_op jit(solution)/shard_map/psum | solution.py:43
  340.8 1.9 slice_negate_fusion
  342.8 0.5 maximum_bitcast_fusion.2
  343.3 0.9 copy-done.1
  344.2 16.4 %fusion.18 = f32[2,2,128,768]{3,2,1,0:T(8,128)} fusion(f32[2,2,128,768]{3,2,1,0:T(8,128)S(1)} %copy-done.1, f32[2,1024,768]{2,1,0:T(8,128)} %param.5, f32[2,2,128,768]{3,2,1,0:T(8,128)S(1)} %bitcast_subtract_fusion.1, f32[2,128]{1,0:T(2,128)S(1)} %div.7, f32[768]{0:T(1024)S(1)} %add_divide_fusion, f32[2,1,2,1024,128]{3,4,0,2,1:T(8,128)S(1)} %get-tuple-element.9, ...), kind=kOutput, calls=%fused_computation.23 | convolution fusion | flops 9666297856 | bytes 15208448 | tf_op jit(solution)/shard_map/pchnb,hng->pcbg/dot_general | solution.py:28
  (24 shorter events, 2.4 us)
Async XLA Ops:
  7.2 333.7 %all-reduce.2.cloned.1.call-start = ((), (), s32[]{:S(2)}) async-start(), calls=%async_computation | async-start | bytes 4194304 | tf_op jit(solution)/shard_map/psum | solution.py:43
  21.2 4.3 %collective-permute-start = (f32[2,2,1024,128]{2,3,0,1:T(8,128)S(1)}, f32[2,2,1024,128]{2,3,0,1:T(8,128)S(1)}, u32[]{:S(2)}, u32[]{:S(2)}) collective-permute-start(f32[2,2,1024,128]{2,3,0,1:T(8,128)S(1)} %pad_maximum_fusion.2), channel_id=1, source_target_pairs={{0,1},{1,0},{2,3},{3,2},{4,5},{5,4},{6,7},{7,6},{8,9},{9,8},{10,11... | collective-permute-start | bytes 6291464 | tf_op jit(solution)/shard_map/ppermute | solution.py:36
  25.9 48.8 %collective-permute-start.1 = (f32[2,2,1024,128]{2,3,0,1:T(8,128)S(1)}, f32[2,2,1024,128]{2,3,0,1:T(8,128)S(1)}, u32[]{:S(2)}, u32[]{:S(2)}) collective-permute-start(f32[2,2,1024,128]{2,3,0,1:T(8,128)S(1)} %fusion.43), channel_id=1, source_target_pairs={{0,2},{1,3},{2,0},{3,1},{4,6},{5,7},{6,4},{7,5},{8,10},{9,11},{10,... | collective-permute-start | bytes 6291464 | tf_op jit(solution)/shard_map/ppermute | solution.py:36
  75.6 50.2 %copy-start.3 = (f32[768]{0:T(1024)S(1)}, f32[768]{0:T(1024)}, u32[]{:S(2)}) copy-start(f32[768]{0:T(1024)} %param.8) | copy-start | bytes 9220
  75.6 47.2 %collective-permute-start.2 = (f32[2,2,1024,128]{2,3,0,1:T(8,128)S(1)}, f32[2,2,1024,128]{2,3,0,1:T(8,128)S(1)}, u32[]{:S(2)}, u32[]{:S(2)}) collective-permute-start(f32[2,2,1024,128]{2,3,0,1:T(8,128)S(1)} %fusion.44), channel_id=1, source_target_pairs={{0,4},{1,5},{2,6},{3,7},{4,0},{5,1},{6,2},{7,3},{8,12},{9,13},{10,... | collective-permute-start | bytes 6291464 | tf_op jit(solution)/shard_map/ppermute | solution.py:36
  123.2 92.1 %collective-permute-start.3 = (f32[2,2,1024,128]{2,3,0,1:T(8,128)S(1)}, f32[2,2,1024,128]{2,3,0,1:T(8,128)S(1)}, u32[]{:S(2)}, u32[]{:S(2)}) collective-permute-start(f32[2,2,1024,128]{2,3,0,1:T(8,128)S(1)} %add.75), channel_id=1, source_target_pairs={{0,8},{1,9},{2,10},{3,11},{4,12},{5,13},{6,14},{7,15},{8,0},{9,1},... | collective-permute-start | bytes 6291464 | tf_op jit(solution)/shard_map/ppermute | solution.py:36
  215.3 2.2 slice-start
  215.7 2.6 slice-start.1
  216.1 2.7 copy-start
  241.5 33.8 %copy-start.4 = (f32[2,128]{1,0:T(2,128)S(1)}, f32[2,128]{1,0:T(2,128)}, u32[]{:S(2)}) copy-start(f32[2,128]{1,0:T(2,128)} %param.9) | copy-start | bytes 3076
  275.3 67.4 %copy-start.2 = (f32[2,128]{1,0:T(2,128)}, f32[2,128]{1,0:T(2,128)S(1)}, u32[]{:S(2)}) copy-start(f32[2,128]{1,0:T(2,128)S(1)} %psum.15) | copy-start | bytes 3076
  342.8 1.4 copy-start.1
Sparse Core Ops, SparseCore 0:
  241.7 99.1 all-reduce.1
